TPU v7x, 128 devices: a whole 4x4x4 slice. The times are simulated.
128 devices in a mesh: dp: 8 (over y, core), fsdp: 16 (over z, x).
Axes of the slice: x: 4, y: 4, z: 4, core: 2. Of those that a mesh axis runs over, the one named last changes fastest.
Arguments:
- grad_q: bfloat16 [8, 8192, 8192], P('dp', 'fsdp'), may hold values from -40 to 40, as said below
- grad_k: bfloat16 [8, 8192, 1024], P('dp', 'fsdp'), may hold values from -40 to 40
- grad_v: bfloat16 [8, 8192, 1024], P('dp', 'fsdp'), may hold values from -40 to 40
- proj_q: bfloat16 [8192, 512], P('fsdp'), may hold values from -5 to 5, as said below
- proj_k: bfloat16 [8192, 512], P('fsdp'), may hold values from -5 to 5
- proj_v: bfloat16 [8192, 512], P('fsdp'), may hold values from -5 to 5
- weight_q: bfloat16 [8192, 8192], P('fsdp', 'dp'), may hold values from -4 to 4
- key_weight_matrix: bfloat16 [8192, 1024], P('fsdp', 'dp'), may hold values from -4 to 4
- value_weight_matrix: bfloat16 [8192, 1024], P('fsdp', 'dp'), may hold values from -4 to 4
- comp_q: bfloat16 [8192, 8192], P('fsdp', 'dp'), may hold values from -0.0039978027 to 0.0039978027
- key_compensation: bfloat16 [8192, 1024], P('fsdp', 'dp'), may hold values from -0.0039978027 to 0.0039978027
- value_compensation: bfloat16 [8192, 1024], P('fsdp', 'dp'), may hold values from -0.0039978027 to 0.0039978027
- avg_q: float32 [512, 8192], P('fsdp', 'dp'), may hold values from -1.5 to 1.5
- key_first_moment: float32 [512, 1024], P('fsdp', 'dp'), may hold values from -1.5 to 1.5
- value_first_moment: float32 [512, 1024], P('fsdp', 'dp'), may hold values from -1.5 to 1.5
- sq_q: float32 [512, 8192], P('fsdp', 'dp'), may hold values from 0.001 to 0.1
- key_second_moment: float32 [512, 1024], P('fsdp', 'dp'), may hold values from 0.001 to 0.1
- value_second_moment: float32 [512, 1024], P('fsdp', 'dp'), may hold values from 0.001 to 0.1
Outputs:
- new_weight_q: float32 [8192, 8192], P('fsdp', 'dp')
- new_weight_k: float32 [8192, 1024], P('fsdp', 'dp')
- new_weight_v: float32 [8192, 1024], P('fsdp', 'dp')
- new_avg_q: float32 [512, 8192], P('fsdp', 'dp')
- new_avg_k: float32 [512, 1024], P('fsdp', 'dp')
- new_avg_v: float32 [512, 1024], P('fsdp', 'dp')
- new_sq_q: float32 [512, 8192], P('fsdp', 'dp')
- new_sq_k: float32 [512, 1024], P('fsdp', 'dp')
- new_sq_v: float32 [512, 1024], P('fsdp', 'dp')
Inputs may be any that keep to these rules, and one draw needn't show every extreme that they name: `grad_q`: each partial of the gradients is real-valued and of full rank. `proj_q`: projectors are real-valued and of full rank 512.
All inputs are finite; a program needn't handle non-finite values.
Results may differ from a plain program's by a relative error of at most 0.00044.
Values may be sent and summed in bfloat16 or wider, within the bound.
No kernel may reach another device: no remote copies, remote signals or barrier semaphores. Data moves between devices by JAX's collectives and lax.ppermute only.
A program may use at most 128 MiB of HBM per device.

v0:
```python
import math
import jax
import jax.numpy as jnp
from jax import lax
from jax.sharding import Mesh
from jax.sharding import PartitionSpec as P

QUERY_OUTPUTS = 8192
KEY_VALUE_OUTS = 1024
PROJECT_RANK = 512
STEP = 10
DP = ("dp_0", "dp_1")
FSDP = ("fsdp_0", "fsdp_1")
DP_FSDP = ("dp_0", "dp_1", "fsdp_0", "fsdp_1")


def in_one_piece(arrays, axis, dim, along):
    both = jnp.concatenate(arrays, axis=along)
    whole, at, done = (lax.psum_scatter(both, axis, scatter_dimension=dim, tiled=True), 0, [])
    for a in arrays:
        done.append(lax.slice_in_dim(whole, at, at + a.shape[along], axis=along))
        at += a.shape[along]
    return tuple(done)


def split_up(x, dim, devices):
    lengths = x.shape
    pieces = x.reshape(*lengths[:dim], devices, lengths[dim] // devices, *lengths[dim + 1 :])
    return jnp.moveaxis(pieces, dim, 0)


def sum_at_owner(x, axis, dim):
    pieces = split_up(x, dim, lax.axis_size(axis))
    arrived = lax.all_to_all(pieces, axis, split_axis=0, concat_axis=0, tiled=True)
    return arrived.sum(axis=0)


def sent_together(arrays, axis, dim, along):
    ends, at = ([], 0)
    for a in arrays[:-1]:
        at += a.shape[along]
        ends.append(at)
    both = jnp.concatenate(arrays, axis=along)
    return tuple(jnp.split(sum_at_owner(both, axis, dim), ends, axis=along))


def over_axes(x, axes):
    for axis in axes:
        x = lax.psum(x, axis)
    return x


def from_everyone(x, axis):
    devices = lax.axis_size(axis)
    return lax.all_to_all(jnp.broadcast_to(x[None], (devices, *x.shape)), axis, 0, 0, tiled=True)


def laid_out(pieces, dim):
    pieces = jnp.moveaxis(pieces, 0, dim)
    lengths = pieces.shape
    return pieces.reshape(*lengths[:dim], lengths[dim] * lengths[dim + 1], *lengths[dim + 2 :])


def gather_directly(x, axis, dim):
    pieces = from_everyone(x, axis)
    return laid_out(pieces, dim)


def side_by_side(arrays, axis, dim, along):
    widths = [a.shape[along] for a in arrays]
    both = jnp.concatenate(arrays, axis=along)
    whole = gather_directly(both, axis, dim)
    return tuple(jnp.split(whole, [sum(widths[:k]) for k in range(1, len(widths))], axis=along))


def adam_apply(projected, clip_factor, first_moment, second_moment):
    scaled = clip_factor * projected
    new_avg = 0.9 * first_moment + 0.1 * scaled
    new_sq = 0.95 * second_moment + 0.05 * scaled * scaled
    correct_one = 1.0 - 0.9**STEP
    correct_two = 1.0 - 0.95**STEP
    update = new_avg / correct_one / (jnp.sqrt(new_sq / correct_two) + 1e-08)
    return (new_avg, new_sq, update.astype(jnp.bfloat16))


def shards(
    grad_q,
    grad_k,
    grad_v,
    proj_q,
    proj_k,
    proj_v,
    weight_q,
    key_weight_matrix,
    value_weight_matrix,
    comp_q,
    key_compensation,
    value_compensation,
    avg_q,
    key_first_moment,
    value_first_moment,
    sq_q,
    key_second_moment,
    value_second_moment,
):
    gradients = (grad_q[0], grad_k[0], grad_v[0])
    projectors = (proj_q, proj_k, proj_v)
    weights = (weight_q, key_weight_matrix, value_weight_matrix)
    comps = (comp_q, key_compensation, value_compensation)
    avgs = (avg_q, key_first_moment, value_first_moment)
    squares = (sq_q, key_second_moment, value_second_moment)
    contract_rows = (((0,), (0,)), ((), ()))
    complete = [
        lax.dot_general(projector, gradient, contract_rows, preferred_element_type=jnp.float32)
        for gradient, projector in zip(gradients, projectors)
    ]
    narrow = (
        lax.psum_scatter(complete[0], DP, scatter_dimension=1, tiled=True),
        *in_one_piece((complete[1], complete[2]), DP, 1, 0),
    )
    shares = sent_together((narrow[0], narrow[1], narrow[2]), FSDP, 0, 1)
    local_sum = jnp.zeros((), jnp.float32)
    for member in shares:
        local_sum = local_sum + jnp.sum(member * member)
    square_sum = over_axes(local_sum, DP_FSDP)
    clipping_threshold = math.sqrt(PROJECT_RANK * (QUERY_OUTPUTS + 2 * KEY_VALUE_OUTS))
    clip_factor = jnp.minimum(1.0, clipping_threshold / jnp.sqrt(square_sum + 1e-06))
    new_avgs, new_sqs, updates = ([], [], [])
    for index_mat in range(3):
        new_avg, new_sq, update = adam_apply(
            shares[index_mat], clip_factor, avgs[index_mat], squares[index_mat]
        )
        new_avgs.append(new_avg)
        new_sqs.append(new_sq)
        updates.append(update)
    zero_sums = tuple((jnp.zeros(weight.shape, jnp.float32) for weight in weights))
    pieces = side_by_side((updates[0], updates[1], updates[2]), FSDP, 0, 1)
    results = []
    for total_acc, piece, projector in zip(zero_sums, pieces, projectors):
        results.append(jnp.dot(projector, piece, preferred_element_type=jnp.float32))
    products = (results[0], results[1], results[2])
    new_weights = []
    for index_mat in range(3):
        delta = -0.04 * products[index_mat]
        new_weights.append(
            weights[index_mat].astype(jnp.float32) + (delta + comps[index_mat].astype(jnp.float32))
        )
    return (
        new_weights[0],
        new_weights[1],
        new_weights[2],
        new_avgs[0],
        new_avgs[1],
        new_avgs[2],
        new_sqs[0],
        new_sqs[1],
        new_sqs[2],
    )


def solution(mesh):
    split = Mesh(mesh.devices.reshape(4, 2, 4, 4), ("dp_0", "dp_1", "fsdp_0", "fsdp_1"))
    return jax.shard_map(
        shards,
        mesh=split,
        in_specs=(
            P(DP, FSDP, None),
            P(DP, FSDP, None),
            P(DP, FSDP, None),
            P(FSDP, None),
            P(FSDP, None),
            P(FSDP, None),
            P(FSDP, DP),
            P(FSDP, DP),
            P(FSDP, DP),
            P(FSDP, DP),
            P(FSDP, DP),
            P(FSDP, DP),
            P(FSDP, DP),
            P(FSDP, DP),
            P(FSDP, DP),
            P(FSDP, DP),
            P(FSDP, DP),
            P(FSDP, DP),
        ),
        out_specs=(
            P(FSDP, DP),
            P(FSDP, DP),
            P(FSDP, DP),
            P(FSDP, DP),
            P(FSDP, DP),
            P(FSDP, DP),
            P(FSDP, DP),
            P(FSDP, DP),
            P(FSDP, DP),
        ),
        check_vma=False,
    )
```

profile of v0, /device:TPU:0, one launch (start us, length us, event | category | flops | bytes accessed | tf_op | source)
XLA Modules:
  0.0 268.8 jit_solution(694423666051327244)
XLA Ops:
  7.3 1.1 copy-done
  8.4 1.8 fusion.10
  10.9 2.5 pad_maximum_fusion
  14.4 11.7 %fusion = f32[512,8192]{1,0:T(8,128)} fusion(bf16[512,512]{1,0:T(8,128)(2,1)S(1)} %copy-done.2, bf16[1,512,8192]{2,1,0:T(8,128)(2,1)} %param.18), kind=kOutput, calls=%fused_computation | convolution fusion | flops 4294967296 | bytes 25690112 | tf_op jit(solution)/shard_map/dot_general | solution.py:114
  26.2 27.8 %reduce-scatter.5.cloned.1.call-done = f32[1024,128]{1,0:T(8,128)} async-done(((f32[1024,1024]{1,0:T(8,128)}), f32[1024,128]{1,0:T(8,128)}) %reduce-scatter.5.cloned.1.call-update) | async-done | bytes 524304 | tf_op jit(solution)/shard_map/reduce_scatter | solution.py:19
  54.0 1.1 fusion.22
  55.1 92.1 %reduce-scatter.3.cloned.1.call-done = f32[512,1024]{1,0:T(8,128)} async-done(((f32[512,8192]{1,0:T(8,128)}), f32[512,1024]{1,0:T(8,128)}) %reduce-scatter.3.cloned.1.call-update) | async-done | bytes 2097168 | tf_op jit(solution)/shard_map/reduce_scatter | solution.py:118
  147.2 1.8 pad_maximum_fusion.1
  149.0 40.4 %all_to_all.10 = f32[16,32,1280]{2,1,0:T(8,128)} all-to-all(f32[16,32,1280]{2,1,0:T(8,128)S(1)} %bitcast.33), channel_id=1, replica_groups=mesh['dp_0'=4,'dp_1'=2,'fsdp_0'=4,'fsdp_1'=4] {'fsdp_0','fsdp_1'}, dimensions={0} | all-to-all | bytes 5242880 | tf_op jit(solution)/shard_map/all_to_all | solution.py:34
  189.5 1.9 reduce_sum.36
  194.6 10.5 %psum.28 = f32[]{:T(128)} all-reduce(f32[]{:T(128)S(6)} %add.70), channel_id=1, replica_groups=mesh['dp_0'=4,'dp_1'=2,'fsdp_0'=4,'fsdp_1'=4] {'dp_0'}, use_global_device_ids=true, to_apply=%region_6.0 | all-reduce | flops 1 | bytes 8 | tf_op jit(solution)/shard_map/psum | solution.py:49
  205.1 3.1 %psum.29 = f32[]{:T(128)} all-reduce(f32[]{:T(128)} %psum.28), channel_id=1, replica_groups=mesh['dp_0'=4,'dp_1'=2,'fsdp_0'=4,'fsdp_1'=4] {'dp_1'}, use_global_device_ids=true, to_apply=%region_7.0 | all-reduce | flops 1 | bytes 8 | tf_op jit(solution)/shard_map/psum | solution.py:49
  208.2 9.2 %psum.30 = f32[]{:T(128)} all-reduce(f32[]{:T(128)} %psum.29), channel_id=1, replica_groups=mesh['dp_0'=4,'dp_1'=2,'fsdp_0'=4,'fsdp_1'=4] {'fsdp_0'}, use_global_device_ids=true, to_apply=%region_8.0 | all-reduce | flops 1 | bytes 8 | tf_op jit(solution)/shard_map/psum | solution.py:49
  217.4 9.7 %psum.31 = f32[]{:T(128)} all-reduce(f32[]{:T(128)} %psum.30), channel_id=1, replica_groups=mesh['dp_0'=4,'dp_1'=2,'fsdp_0'=4,'fsdp_1'=4] {'fsdp_1'}, use_global_device_ids=true, to_apply=%region_9.0 | all-reduce | flops 1 | bytes 8 | tf_op jit(solution)/shard_map/psum | solution.py:49
  229.2 1.2 broadcast_in_dim.2
  230.4 3.7 %all-to-all-start.1 = ((bf16[16,32,1280]{2,1,0:T(8,128)(2,1)}), bf16[16,32,1280]{2,1,0:T(8,128)(2,1)S(1)}, u32[]{:S(2)}, u32[]{:S(2)}) async-start(bf16[16,32,1280]{2,1,0:T(8,128)(2,1)} %broadcast_in_dim.2), calls=%async_computation.3 | async-start | bytes 2621440 | tf_op jit(solution)/shard_map/all_to_all | solution.py:55
  234.1 1.3 copy.27
  235.5 2.4 copy.28
  239.0 12.6 %all-to-all-done.1 = bf16[16,32,1280]{2,1,0:T(8,128)(2,1)S(1)} async-done(((bf16[16,32,1280]{2,1,0:T(8,128)(2,1)}), bf16[16,32,1280]{2,1,0:T(8,128)(2,1)S(1)}, u32[]{:S(2)}, u32[]{:S(2)}) %all-to-all-start.1) | async-done | bytes 1310752 | tf_op jit(solution)/shard_map/all_to_all | solution.py:55
  251.6 1.1 copy-done.1
  252.7 2.9 %fusion.2 = f32[512,1024]{0,1:T(8,128)S(1)} fusion(bf16[512,1024]{0,1:T(8,128)(2,1)} %copy.28, bf16[512,1024]{0,1:T(8,128)(2,1)} %copy.27, bf16[512,512]{1,0:T(8,128)(2,1)} %param.21, bf16[512,1280]{1,0:T(8,128)(2,1)} %bitcast.34), kind=kOutput, calls=%fused_computation.5 | convolution fusion | flops 539492352 | bytes 5767168 | tf_op jit(solution)/shard_map/dot_general | solution.py:140
  255.6 1.8 copy.33
  257.4 1.4 fusion.8
  259.6 1.4 fusion.7
  (46 shorter events, 7.3 us)
Async XLA Ops:
  7.2 1.2 copy-start
  7.2 3.0 %copy-start.4 = (bf16[1,512,1024]{2,1,0:T(8,128)(2,1)S(1)}, bf16[1,512,1024]{2,1,0:T(8,128)(2,1)}, u32[]{:S(2)}) copy-start(bf16[1,512,1024]{2,1,0:T(8,128)(2,1)} %param.19) | copy-start | bytes 3145732
  7.2 3.0 %copy-start.3 = (bf16[512,512]{1,0:T(8,128)(2,1)S(1)}, bf16[512,512]{1,0:T(8,128)(2,1)}, u32[]{:S(2)}) copy-start(bf16[512,512]{1,0:T(8,128)(2,1)} %param.22) | copy-start | bytes 1572868
  7.2 46.8 %reduce-scatter.5.cloned.1.call-start = ((), (), s32[]{:S(2)}) async-start(), calls=%async_computation.5 | async-start | bytes 4718592 | tf_op jit(solution)/shard_map/reduce_scatter | solution.py:19
  13.4 1.0 copy-start.2
  13.4 133.8 %reduce-scatter.3.cloned.1.call-start = ((), (), s32[]{:S(2)}) async-start(), calls=%async_computation.4 | async-start | bytes 18874368 | tf_op jit(solution)/shard_map/reduce_scatter | solution.py:118
  189.4 38.3 %copy-start.6 = (f32[32,1024]{1,0:T(8,128)S(1)}, f32[32,1024]{1,0:T(8,128)}, u32[]{:S(2)}) copy-start(f32[32,1024]{1,0:T(8,128)} %param.30) | copy-start | bytes 393220
  189.4 38.3 %copy-start.7 = (f32[32,1024]{1,0:T(8,128)S(1)}, f32[32,1024]{1,0:T(8,128)}, u32[]{:S(2)}) copy-start(f32[32,1024]{1,0:T(8,128)} %param.33) | copy-start | bytes 393220
  189.4 39.1 %copy-start.12 = (f32[32,128]{1,0:T(8,128)S(1)}, f32[32,128]{1,0:T(8,128)}, u32[]{:S(2)}) copy-start(f32[32,128]{1,0:T(8,128)} %param.31) | copy-start | bytes 49156
  189.5 39.1 %copy-start.13 = (f32[32,128]{1,0:T(8,128)S(1)}, f32[32,128]{1,0:T(8,128)}, u32[]{:S(2)}) copy-start(f32[32,128]{1,0:T(8,128)} %param.34) | copy-start | bytes 49156
  189.5 39.1 %copy-start.14 = (f32[32,128]{1,0:T(8,128)S(1)}, f32[32,128]{1,0:T(8,128)}, u32[]{:S(2)}) copy-start(f32[32,128]{1,0:T(8,128)} %param.35) | copy-start | bytes 49156
  189.5 39.1 %copy-start.15 = (f32[32,128]{1,0:T(8,128)S(1)}, f32[32,128]{1,0:T(8,128)}, u32[]{:S(2)}) copy-start(f32[32,128]{1,0:T(8,128)} %param.32) | copy-start | bytes 49156
  229.2 4.9 %copy-start.5 = (bf16[512,1024]{1,0:T(8,128)(2,1)S(1)}, bf16[512,1024]{1,0:T(8,128)(2,1)}, u32[]{:S(2)}) copy-start(bf16[512,1024]{1,0:T(8,128)(2,1)} %param.24) | copy-start | bytes 3145732
  230.4 21.2 %all-to-all-start.1 = ((bf16[16,32,1280]{2,1,0:T(8,128)(2,1)}), bf16[16,32,1280]{2,1,0:T(8,128)(2,1)S(1)}, u32[]{:S(2)}, u32[]{:S(2)}) async-start(bf16[16,32,1280]{2,1,0:T(8,128)(2,1)} %broadcast_in_dim.2), calls=%async_computation.3 | async-start | bytes 2621440 | tf_op jit(solution)/shard_map/all_to_all | solution.py:55
  235.5 2.4 copy-start.8
  235.5 2.5 copy-start.9
  235.5 3.3 %copy-start.10 = (bf16[512,128]{1,0:T(8,128)(2,1)S(1)}, bf16[512,128]{1,0:T(8,128)(2,1)}, u32[]{:S(2)}) copy-start(bf16[512,128]{1,0:T(8,128)(2,1)} %param.26) | copy-start | bytes 393220
  235.5 3.4 %copy-start.11 = (bf16[512,128]{1,0:T(8,128)(2,1)S(1)}, bf16[512,128]{1,0:T(8,128)(2,1)}, u32[]{:S(2)}) copy-start(bf16[512,128]{1,0:T(8,128)(2,1)} %param.29) | copy-start | bytes 393220
  251.6 1.1 copy-start.1
Sparse Core Ops, SparseCore 0:
  13.5 40.4 reduce-scatter.4
  56.5 90.6 reduce-scatter.2
where the time goes:
time: 269 us
  waiting for transfers between devices  133 us (49%)
  blocking collectives  72.9 us (27%)
  matrix products  20 us (7%)
  between operations  16.9 us (6%)
  local copies, waits for them, and re-layouts  13.8 us (5%)
  other arithmetic  8.86 us (3%)
  starting transfers between devices  3.78 us (1%)
    reduce_scatter x1, waiting for transfers between devices, shards(): lax.psum_scatter(complete[0], DP, scatter_dimension=1, tiled=True)  92.1 us
    all_to_all x1, blocking collectives, sum_at_owner(): lax.all_to_all(pieces, axis, split_axis=0, concat_axis=0, tiled=True)  40.4 us
    psum x4, blocking collectives, over_axes(): x = lax.psum(x, axis)  32.5 us
    reduce_scatter x1, waiting for transfers between devices, in_one_piece(): lax.psum_scatter(both, axis, scatter_dimension=dim, tiled=True)  27.8 us
    dot_general x3, matrix products, shards(): lax.dot_general(projector, gradient, contract_rows, preferred_element_typ...  14.2 us
    all_to_all x1, waiting for transfers between devices, from_everyone(): lax.all_to_all(jnp.broadcast_to(x[None], (devices, *x.shape)), axis, 0, 0...  12.6 us
    unnamed x41, local copies, waits for them, and re-layouts  11.5 us
    dot_general x3, matrix products, shards(): jnp.dot(projector, piece, preferred_element_type=jnp.float32)  5.74 us
  transfers between devices with their start and end apart: 3, of which 3 were waited for; matrix products, arithmetic and copies ran while one was open for 7% of the time, Pallas kernels for 0%

commit v1 on v0

--- a/solution.py
+++ b/solution.py
@@ -46,7 +46,7 @@
 
 def over_axes(x, axes):
     for axis in axes:
-        x = lax.psum(x, axis)
+        x = jnp.sum(lax.all_gather(x, axis), axis=0)
     return x
 
 

time: 269 us -> 285 us (1.059)
  blocking collectives: 72.9 us -> 32.5 us
  waiting for transfers between devices: 133 us -> 170 us
  local copies, waits for them, and re-layouts: 13.8 us -> 21.1 us
  starting transfers between devices: 3.78 us -> 10.9 us
  other arithmetic: 8.86 us -> 12.7 us
    all_to_all x1 -> x0, blocking collectives: 40.4 us -> none  [sum_at_owner(): lax.all_to_all(pieces, axis, split_axis=0, concat_axis=0, tiled=True)]
    all_to_all x0 -> x1, waiting for transfers between devices: none -> 37.4 us  [sum_at_owner(): lax.all_to_all(pieces, axis, split_axis=0, concat_axis=0, tiled=True)]
    unnamed x0 -> x4, blocking collectives: none -> 32.5 us
    psum x4 -> x0, blocking collectives: 32.5 us -> none  [over_axes(): x = lax.psum(x, axis)]
    unnamed x41 -> x61, local copies, waits for them, and re-layouts: 11.5 us -> 18.9 us
    all_to_all x0 -> x1, starting transfers between devices: none -> 7.11 us  [sum_at_owner(): lax.all_to_all(pieces, axis, split_axis=0, concat_axis=0, tiled=True)]
  transfers between devices with their start and end apart: 3 -> 4, of which waited for: 3 -> 4; matrix products, arithmetic and copies ran while one was open for 7% -> 6% of each run, Pallas kernels for 0% -> 0%
where the time goes in v1:
time: 285 us; the launch traced here: 284 us
  waiting for transfers between devices  170 us (60%)
  blocking collectives  32.5 us (11%)
  local copies, waits for them, and re-layouts  21.1 us (7%)
  matrix products  20 us (7%)
  between operations  17 us (6%)
  other arithmetic  12.7 us (4%)
  starting transfers between devices  10.9 us (4%)
    reduce_scatter x1, waiting for transfers between devices, shards(): lax.psum_scatter(complete[0], DP, scatter_dimension=1, tiled=True)  92.1 us
    all_to_all x1, waiting for transfers between devices, sum_at_owner(): lax.all_to_all(pieces, axis, split_axis=0, concat_axis=0, tiled=True)  37.4 us
    unnamed x4, blocking collectives  32.5 us
    reduce_scatter x1, waiting for transfers between devices, in_one_piece(): lax.psum_scatter(both, axis, scatter_dimension=dim, tiled=True)  27.8 us
    unnamed x61, local copies, waits for them, and re-layouts  18.9 us
    dot_general x3, matrix products, shards(): lax.dot_general(projector, gradient, contract_rows, preferred_element_typ...  14.2 us
    all_to_all x1, waiting for transfers between devices, from_everyone(): lax.all_to_all(jnp.broadcast_to(x[None], (devices, *x.shape)), axis, 0, 0...  12.6 us
    all_to_all x1, starting transfers between devices, sum_at_owner(): lax.all_to_all(pieces, axis, split_axis=0, concat_axis=0, tiled=True)  7.11 us
  transfers between devices with their start and end apart: 4, of which 4 were waited for; matrix products, arithmetic and copies ran while one was open for 6% of the time, Pallas kernels for 0%

profile of v1, /device:TPU:0, one launch (start us, length us, event | category | flops | bytes accessed | tf_op | source)
XLA Modules:
  0.0 284.2 jit_solution(11848032724694421629)
XLA Ops:
  8.4 1.8 fusion.10
  10.9 2.5 pad_maximum_fusion
  14.4 11.7 %fusion = f32[512,8192]{1,0:T(8,128)} fusion(bf16[512,512]{1,0:T(8,128)(2,1)S(1)} %copy-done.2, bf16[1,512,8192]{2,1,0:T(8,128)(2,1)} %param.18), kind=kOutput, calls=%fused_computation | convolution fusion | flops 4294967296 | bytes 25690112 | tf_op jit(solution)/shard_map/dot_general | solution.py:114
  26.2 27.8 %reduce-scatter.5.cloned.1.call-done = f32[1024,128]{1,0:T(8,128)} async-done(((f32[1024,1024]{1,0:T(8,128)}), f32[1024,128]{1,0:T(8,128)}) %reduce-scatter.5.cloned.1.call-update) | async-done | bytes 524304 | tf_op jit(solution)/shard_map/reduce_scatter | solution.py:19
  55.1 92.1 %reduce-scatter.3.cloned.1.call-done = f32[512,1024]{1,0:T(8,128)} async-done(((f32[512,8192]{1,0:T(8,128)}), f32[512,1024]{1,0:T(8,128)}) %reduce-scatter.3.cloned.1.call-update) | async-done | bytes 2097168 | tf_op jit(solution)/shard_map/reduce_scatter | solution.py:118
  147.2 3.3 %pad_maximum_fusion.1 = f32[512,1280]{1,0:T(8,128)} fusion(f32[512,128]{1,0:T(8,128)S(1)} %get-tuple-element.30, f32[512,128]{1,0:T(8,128)S(1)} %get-tuple-element.29, f32[512,1024]{1,0:T(8,128)} %reduce-scatter.3.cloned.1.call-done), kind=kLoop, calls=%fused_computation.3 | loop fusion | flops 1310720 | bytes 5242880 | tf_op jit(solution)/shard_map/concatenate | solution.py:43
  150.5 7.1 %all-to-all-start = ((f32[16,32,1280]{2,1,0:T(8,128)}), f32[16,32,1280]{2,1,0:T(8,128)}, u32[]{:S(2)}, u32[]{:S(2)}) async-start(f32[16,32,1280]{2,1,0:T(8,128)} %bitcast.41), calls=%async_computation.2 | async-start | bytes 5242880 | tf_op jit(solution)/shard_map/all_to_all | solution.py:34
  158.4 37.4 %all-to-all-done = f32[16,32,1280]{2,1,0:T(8,128)} async-done(((f32[16,32,1280]{2,1,0:T(8,128)}), f32[16,32,1280]{2,1,0:T(8,128)}, u32[]{:S(2)}, u32[]{:S(2)}) %all-to-all-start) | async-done | bytes 2621472 | tf_op jit(solution)/shard_map/all_to_all | solution.py:34
  195.8 1.9 reduce_sum.72
  202.2 12.1 %all-reduce = f32[4]{0:T(128)S(1)} all-reduce(f32[4]{0:T(128)S(1)} %dynamic-update-slice), channel_id=1, replica_groups=mesh['dp_0'=4,'dp_1'=2,'fsdp_0'=4,'fsdp_1'=4] {'dp_0'}, use_global_device_ids=true, to_apply=%add | all-reduce | flops 4 | bytes 32
  214.9 1.4 dynamic-update-slice.1
  216.9 2.4 all-reduce.1
  219.9 1.4 dynamic-update-slice.2
  221.9 9.3 %all-reduce.2 = f32[4]{0:T(128)S(1)} all-reduce(f32[4]{0:T(128)S(1)} %dynamic-update-slice.2), channel_id=1, replica_groups=mesh['dp_0'=4,'dp_1'=2,'fsdp_0'=4,'fsdp_1'=4] {'fsdp_0'}, use_global_device_ids=true, to_apply=%add.2 | all-reduce | flops 4 | bytes 32
  231.8 1.4 dynamic-update-slice.3
  233.2 8.7 %all-reduce.3 = f32[4]{0:T(128)S(1)} all-reduce(f32[4]{0:T(128)S(1)} %dynamic-update-slice.3), channel_id=1, replica_groups=mesh['dp_0'=4,'dp_1'=2,'fsdp_0'=4,'fsdp_1'=4] {'fsdp_1'}, use_global_device_ids=true, to_apply=%add.3 | all-reduce | flops 4 | bytes 32
  245.9 3.7 %all-to-all-start.1 = ((bf16[16,32,1280]{2,1,0:T(8,128)(2,1)}), bf16[16,32,1280]{2,1,0:T(8,128)(2,1)S(1)}, u32[]{:S(2)}, u32[]{:S(2)}) async-start(bf16[16,32,1280]{2,1,0:T(8,128)(2,1)} %broadcast_in_dim.2), calls=%async_computation.3 | async-start | bytes 2621440 | tf_op jit(solution)/shard_map/all_to_all | solution.py:55
  249.6 1.3 copy.27
  250.9 2.4 copy.28
  254.4 12.6 %all-to-all-done.1 = bf16[16,32,1280]{2,1,0:T(8,128)(2,1)S(1)} async-done(((bf16[16,32,1280]{2,1,0:T(8,128)(2,1)}), bf16[16,32,1280]{2,1,0:T(8,128)(2,1)S(1)}, u32[]{:S(2)}, u32[]{:S(2)}) %all-to-all-start.1) | async-done | bytes 1310752 | tf_op jit(solution)/shard_map/all_to_all | solution.py:55
  268.1 2.9 %fusion.2 = f32[512,1024]{0,1:T(8,128)S(1)} fusion(bf16[512,1024]{0,1:T(8,128)(2,1)} %copy.28, bf16[512,1024]{0,1:T(8,128)(2,1)} %copy.27, bf16[512,512]{1,0:T(8,128)(2,1)} %param.21, bf16[512,1280]{1,0:T(8,128)(2,1)} %bitcast.42), kind=kOutput, calls=%fused_computation.5 | convolution fusion | flops 539492352 | bytes 5767168 | tf_op jit(solution)/shard_map/dot_general | solution.py:140
  271.0 1.8 copy.33
  272.8 1.4 fusion.8
  275.1 1.4 fusion.7
  (71 shorter events, 17.3 us)
Async XLA Ops:
  7.2 1.2 copy-start
  7.2 3.0 %copy-start.4 = (bf16[1,512,1024]{2,1,0:T(8,128)(2,1)S(1)}, bf16[1,512,1024]{2,1,0:T(8,128)(2,1)}, u32[]{:S(2)}) copy-start(bf16[1,512,1024]{2,1,0:T(8,128)(2,1)} %param.19) | copy-start | bytes 3145732
  7.2 3.0 %copy-start.3 = (bf16[512,512]{1,0:T(8,128)(2,1)S(1)}, bf16[512,512]{1,0:T(8,128)(2,1)}, u32[]{:S(2)}) copy-start(bf16[512,512]{1,0:T(8,128)(2,1)} %param.22) | copy-start | bytes 1572868
  7.2 46.8 %reduce-scatter.5.cloned.1.call-start = ((), (), s32[]{:S(2)}) async-start(), calls=%async_computation.5 | async-start | bytes 4718592 | tf_op jit(solution)/shard_map/reduce_scatter | solution.py:19
  13.4 1.0 copy-start.2
  13.4 133.8 %reduce-scatter.3.cloned.1.call-start = ((), (), s32[]{:S(2)}) async-start(), calls=%async_computation.4 | async-start | bytes 18874368 | tf_op jit(solution)/shard_map/reduce_scatter | solution.py:118
  150.5 7.2 %copy-start.19 = (u32[128]{0:T(128)S(1)}, u32[128]{0:T(128)}, u32[]{:S(2)}) copy-start(u32[128]{0:T(128)} %constant.43) | copy-start | bytes 1540
  150.5 45.2 %all-to-all-start = ((f32[16,32,1280]{2,1,0:T(8,128)}), f32[16,32,1280]{2,1,0:T(8,128)}, u32[]{:S(2)}, u32[]{:S(2)}) async-start(f32[16,32,1280]{2,1,0:T(8,128)} %bitcast.41), calls=%async_computation.2 | async-start | bytes 5242880 | tf_op jit(solution)/shard_map/all_to_all | solution.py:34
  157.7 43.9 %copy-start.18 = (u32[128]{0:T(128)S(1)}, u32[128]{0:T(128)}, u32[]{:S(2)}) copy-start(u32[128]{0:T(128)} %constant.48) | copy-start | bytes 1540
  157.7 58.6 %copy-start.17 = (u32[128]{0:T(128)S(1)}, u32[128]{0:T(128)}, u32[]{:S(2)}) copy-start(u32[128]{0:T(128)} %constant.53) | copy-start | bytes 1540
  157.7 63.6 %copy-start.16 = (u32[128]{0:T(128)S(1)}, u32[128]{0:T(128)}, u32[]{:S(2)}) copy-start(u32[128]{0:T(128)} %constant.58) | copy-start | bytes 1540
  157.7 85.5 %copy-start.6 = (f32[32,1024]{1,0:T(8,128)S(1)}, f32[32,1024]{1,0:T(8,128)}, u32[]{:S(2)}) copy-start(f32[32,1024]{1,0:T(8,128)} %param.30) | copy-start | bytes 393220
  157.7 85.5 %copy-start.7 = (f32[32,1024]{1,0:T(8,128)S(1)}, f32[32,1024]{1,0:T(8,128)}, u32[]{:S(2)}) copy-start(f32[32,1024]{1,0:T(8,128)} %param.33) | copy-start | bytes 393220
  157.7 86.3 %copy-start.12 = (f32[32,128]{1,0:T(8,128)S(1)}, f32[32,128]{1,0:T(8,128)}, u32[]{:S(2)}) copy-start(f32[32,128]{1,0:T(8,128)} %param.31) | copy-start | bytes 49156
  157.7 86.3 %copy-start.13 = (f32[32,128]{1,0:T(8,128)S(1)}, f32[32,128]{1,0:T(8,128)}, u32[]{:S(2)}) copy-start(f32[32,128]{1,0:T(8,128)} %param.34) | copy-start | bytes 49156
  157.7 86.3 %copy-start.14 = (f32[32,128]{1,0:T(8,128)S(1)}, f32[32,128]{1,0:T(8,128)}, u32[]{:S(2)}) copy-start(f32[32,128]{1,0:T(8,128)} %param.35) | copy-start | bytes 49156
  157.8 86.3 %copy-start.15 = (f32[32,128]{1,0:T(8,128)S(1)}, f32[32,128]{1,0:T(8,128)}, u32[]{:S(2)}) copy-start(f32[32,128]{1,0:T(8,128)} %param.32) | copy-start | bytes 49156
  244.7 4.9 %copy-start.5 = (bf16[512,1024]{1,0:T(8,128)(2,1)S(1)}, bf16[512,1024]{1,0:T(8,128)(2,1)}, u32[]{:S(2)}) copy-start(bf16[512,1024]{1,0:T(8,128)(2,1)} %param.24) | copy-start | bytes 3145732
  245.9 21.2 %all-to-all-start.1 = ((bf16[16,32,1280]{2,1,0:T(8,128)(2,1)}), bf16[16,32,1280]{2,1,0:T(8,128)(2,1)S(1)}, u32[]{:S(2)}, u32[]{:S(2)}) async-start(bf16[16,32,1280]{2,1,0:T(8,128)(2,1)} %broadcast_in_dim.2), calls=%async_computation.3 | async-start | bytes 2621440 | tf_op jit(solution)/shard_map/all_to_all | solution.py:55
  250.9 2.4 copy-start.8
  250.9 2.5 copy-start.9
  250.9 3.3 %copy-start.10 = (bf16[512,128]{1,0:T(8,128)(2,1)S(1)}, bf16[512,128]{1,0:T(8,128)(2,1)}, u32[]{:S(2)}) copy-start(bf16[512,128]{1,0:T(8,128)(2,1)} %param.26) | copy-start | bytes 393220
  250.9 3.4 %copy-start.11 = (bf16[512,128]{1,0:T(8,128)(2,1)S(1)}, bf16[512,128]{1,0:T(8,128)(2,1)}, u32[]{:S(2)}) copy-start(bf16[512,128]{1,0:T(8,128)(2,1)} %param.29) | copy-start | bytes 393220
  267.0 1.1 copy-start.1
Sparse Core Ops, SparseCore 0:
  13.5 40.4 reduce-scatter.4
  56.5 90.6 reduce-scatter.2
